TPU v7x, 512 devices: a whole 4x4x16 slice. The times are simulated.
512 devices in a mesh: row: 16 (over y_lo, x, core), col: 32 (over z, y_hi).
Axes of the slice: x: 4, y: 4 (y_hi: 2, y_lo: 2; y = y_hi * 2 + y_lo), z: 16, core: 2. Of those that a mesh axis runs over, the one named last changes fastest.
Arguments:
- users: bfloat16 [524288, 256], P(('row', 'col')), may hold values from -20 to 20
- positives: int32 [524288], P(('row', 'col')), may hold values from 0 to 8191
- items: bfloat16 [8192, 256], P(('row', 'col')), may hold values from -6 to 6
- item_ids: int32 [8192], P(('row', 'col')), may hold values from 0 to 999999
Outputs:
- loss: float32 [524288], P(('row', 'col'))
All inputs are finite; a program needn't handle non-finite values.
Results may differ from a plain program's by a relative error of at most 0.0003.
Values may be sent and summed in bfloat16 or wider, within the bound.
A program may use at most 128 MiB of HBM per device.

v0:
```python
import jax
import jax.numpy as jnp
from jax import lax
from jax.sharding import PartitionSpec as P


def copy_for_each(value, axis):
    size = lax.axis_size(axis)
    return lax.all_to_all(
        jnp.broadcast_to(value[None], (size, *value.shape)), axis, 0, 0, tiled=True
    )


def in_order(parts, dim):
    dims = list(parts.shape[1:])
    dims[dim] *= parts.shape[0]
    return jnp.moveaxis(parts, 0, dim).reshape(dims)


def gathered_copies(value, axis, dim):
    parts = copy_for_each(value, axis)
    return in_order(parts, dim)


def shifted(value, axis, by):
    size = lax.axis_size(axis)
    return lax.ppermute(value, axis, [(i, (i + by) % size) for i in range(size)])


def absorb(carry, users, positives, pos_id, table, piece, where_at):
    high, summed, chosen = carry
    scores = 0.125 * lax.dot_general(
        users, piece, (((1,), (1,)), ((), ())), preferred_element_type=jnp.float32
    )
    ids = jnp.take(table, where_at)
    hit = where_at[None, :] == positives[:, None]
    keep = (ids[None, :] != pos_id[:, None]) | hit
    masked = jnp.where(keep, scores, -1e30)
    new_high = jnp.maximum(high, jnp.max(masked, axis=1))
    terms = jnp.where(keep, jnp.exp(masked - new_high[:, None]), 0.0)
    summed = summed * jnp.exp(high - new_high) + jnp.sum(terms, axis=1)
    chosen = chosen + jnp.sum(jnp.where(hit, scores, 0.0), axis=1)
    return (new_high, summed, chosen)


def body(users, positives, items, item_ids):
    table = lax.all_gather(item_ids, ("row", "col"), axis=0, tiled=True)
    pos_id = jnp.take(table, positives)
    user_rows = users.shape[0]
    per_device = items.shape[0]
    col_count = lax.axis_size("col")
    row_count = lax.axis_size("row")
    init = (
        jnp.full((user_rows,), -1e30, jnp.float32),
        jnp.zeros((user_rows,), jnp.float32),
        jnp.zeros((user_rows,), jnp.float32),
    )

    def sweep_col(block, source_row, carry):
        piece = gathered_copies(block, "col", 0)
        where_at = source_row * col_count * per_device + jnp.arange(piece.shape[0], dtype=jnp.int32)
        return absorb(carry, users, positives, pos_id, table, piece, where_at)

    own_row = lax.axis_index("row")
    carry = sweep_col(items, own_row, init)

    def cycle_turn(turn, state):
        block, inner = state
        block = shifted(block, "row", 1)
        source_row = (own_row - turn) % row_count
        return (block, sweep_col(block, source_row, inner))

    _, carry = lax.fori_loop(1, row_count, cycle_turn, (items, carry))
    high, summed, chosen = carry
    return high + jnp.log(summed) - chosen


def solution(mesh):
    in_specs = (
        P(("row", "col"), None),
        P(("row", "col")),
        P(("row", "col"), None),
        P(("row", "col")),
    )
    out_specs = P(("row", "col"))
    return jax.shard_map(body, mesh=mesh, in_specs=in_specs, out_specs=out_specs, check_vma=False)
```

profile of v0, /device:TPU:6, one launch (start us, length us, event | category | flops | bytes accessed | tf_op | source)
XLA Modules:
  0.0 639.8 jit_solution(12506163252631837681)
XLA Ops:
  1.4 18.1 %all-to-all-start.1 = ((bf16[32,16,256]{2,1,0:T(8,128)(2,1)}), bf16[32,16,256]{2,1,0:T(8,128)(2,1)S(1)}, u32[]{:S(2)}, u32[]{:S(2)}) async-start(bf16[32,16,256]{2,1,0:T(8,128)(2,1)} %broadcast_in_dim.96), calls=%async_computation.1 | async-start | bytes 524288 | tf_op jit(solution)/shard_map/all_to_all | solution.py:9
  20.4 103.9 %all-reduce = s32[8192]{0:T(1024)S(1)} all-reduce(s32[8192]{0:T(1024)S(1)} %dynamic-update-slice), channel_id=1, replica_groups=mesh['row'=16,'col'=32] {'row','col'}, use_global_device_ids=true, to_apply=%add | all-reduce | flops 8192 | bytes 65536
  127.6 6.2 gather_fusion.1
  135.4 503.8 %while.21 = (s32[]{:T(128)}, bf16[16,256]{1,0:T(8,128)(2,1)S(1)}, f32[1024]{0:T(1024)S(1)}, f32[1024]{0:T(1024)S(1)}, f32[1024]{0:T(1024)S(1)}, /*index=5*/s32[]...) while((s32[]{:T(128)}, bf16[16,256]{1,0:T(8,128)(2,1)S(1)}, ...), condition=%wide.region_7.9_spmd, body=%wide.region_3.8_spmd.sunk | while | flops 276833280 | bytes 6201698 | solution.py:73
  141.1 9.1 %all-to-all-start = ((bf16[32,16,256]{2,1,0:T(8,128)(2,1)}), bf16[32,16,256]{2,1,0:T(8,128)(2,1)S(1)}, u32[]{:S(2)}, u32[]{:S(2)}) async-start(bf16[32,16,256]{2,1,0:T(8,128)(2,1)} %broadcast_in_dim.128), calls=%async_computation | async-start | bytes 524288 | tf_op jit(solution)/shard_map/while/body/eval_jaxpr/all_to_all | solution.py:9
  150.2 3.1 gather_fusion
  153.4 20.0 %all-to-all-done = bf16[32,16,256]{2,1,0:T(8,128)(2,1)S(1)} async-done(((bf16[32,16,256]{2,1,0:T(8,128)(2,1)}), bf16[32,16,256]{2,1,0:T(8,128)(2,1)S(1)}, u32[]{:S(2)}, u32[]{:S(2)}) %all-to-all-start) | async-done | bytes 262176 | tf_op jit(solution)/shard_map/while/body/eval_jaxpr/all_to_all | solution.py:9
  180.7 4.7 all-to-all-start
  185.5 3.1 gather_fusion
  188.7 17.4 %all-to-all-done = bf16[32,16,256]{2,1,0:T(8,128)(2,1)S(1)} async-done(((bf16[32,16,256]{2,1,0:T(8,128)(2,1)}), bf16[32,16,256]{2,1,0:T(8,128)(2,1)S(1)}, u32[]{:S(2)}, u32[]{:S(2)}) %all-to-all-start) | async-done | bytes 262176 | tf_op jit(solution)/shard_map/while/body/eval_jaxpr/all_to_all | solution.py:9
  213.4 4.8 all-to-all-start
  218.2 3.1 gather_fusion
  221.3 16.9 %all-to-all-done = bf16[32,16,256]{2,1,0:T(8,128)(2,1)S(1)} async-done(((bf16[32,16,256]{2,1,0:T(8,128)(2,1)}), bf16[32,16,256]{2,1,0:T(8,128)(2,1)S(1)}, u32[]{:S(2)}, u32[]{:S(2)}) %all-to-all-start) | async-done | bytes 262176 | tf_op jit(solution)/shard_map/while/body/eval_jaxpr/all_to_all | solution.py:9
  245.6 4.8 all-to-all-start
  250.4 3.1 gather_fusion
  253.6 17.8 %all-to-all-done = bf16[32,16,256]{2,1,0:T(8,128)(2,1)S(1)} async-done(((bf16[32,16,256]{2,1,0:T(8,128)(2,1)}), bf16[32,16,256]{2,1,0:T(8,128)(2,1)S(1)}, u32[]{:S(2)}, u32[]{:S(2)}) %all-to-all-start) | async-done | bytes 262176 | tf_op jit(solution)/shard_map/while/body/eval_jaxpr/all_to_all | solution.py:9
  278.7 4.8 all-to-all-start
  283.5 3.1 gather_fusion
  286.7 19.3 %all-to-all-done = bf16[32,16,256]{2,1,0:T(8,128)(2,1)S(1)} async-done(((bf16[32,16,256]{2,1,0:T(8,128)(2,1)}), bf16[32,16,256]{2,1,0:T(8,128)(2,1)S(1)}, u32[]{:S(2)}, u32[]{:S(2)}) %all-to-all-start) | async-done | bytes 262176 | tf_op jit(solution)/shard_map/while/body/eval_jaxpr/all_to_all | solution.py:9
  313.3 4.8 all-to-all-start
  318.2 3.1 gather_fusion
  321.4 17.3 %all-to-all-done = bf16[32,16,256]{2,1,0:T(8,128)(2,1)S(1)} async-done(((bf16[32,16,256]{2,1,0:T(8,128)(2,1)}), bf16[32,16,256]{2,1,0:T(8,128)(2,1)S(1)}, u32[]{:S(2)}, u32[]{:S(2)}) %all-to-all-start) | async-done | bytes 262176 | tf_op jit(solution)/shard_map/while/body/eval_jaxpr/all_to_all | solution.py:9
  346.0 4.8 all-to-all-start
  350.8 3.1 gather_fusion
  353.9 17.4 %all-to-all-done = bf16[32,16,256]{2,1,0:T(8,128)(2,1)S(1)} async-done(((bf16[32,16,256]{2,1,0:T(8,128)(2,1)}), bf16[32,16,256]{2,1,0:T(8,128)(2,1)S(1)}, u32[]{:S(2)}, u32[]{:S(2)}) %all-to-all-start) | async-done | bytes 262176 | tf_op jit(solution)/shard_map/while/body/eval_jaxpr/all_to_all | solution.py:9
  378.6 4.8 all-to-all-start
  383.5 3.1 gather_fusion
  386.6 17.8 %all-to-all-done = bf16[32,16,256]{2,1,0:T(8,128)(2,1)S(1)} async-done(((bf16[32,16,256]{2,1,0:T(8,128)(2,1)}), bf16[32,16,256]{2,1,0:T(8,128)(2,1)S(1)}, u32[]{:S(2)}, u32[]{:S(2)}) %all-to-all-start) | async-done | bytes 262176 | tf_op jit(solution)/shard_map/while/body/eval_jaxpr/all_to_all | solution.py:9
  411.8 4.8 all-to-all-start
  416.6 3.1 gather_fusion
  419.7 20.1 %all-to-all-done = bf16[32,16,256]{2,1,0:T(8,128)(2,1)S(1)} async-done(((bf16[32,16,256]{2,1,0:T(8,128)(2,1)}), bf16[32,16,256]{2,1,0:T(8,128)(2,1)S(1)}, u32[]{:S(2)}, u32[]{:S(2)}) %all-to-all-start) | async-done | bytes 262176 | tf_op jit(solution)/shard_map/while/body/eval_jaxpr/all_to_all | solution.py:9
  447.2 4.7 all-to-all-start
  451.9 3.1 gather_fusion
  455.1 17.2 %all-to-all-done = bf16[32,16,256]{2,1,0:T(8,128)(2,1)S(1)} async-done(((bf16[32,16,256]{2,1,0:T(8,128)(2,1)}), bf16[32,16,256]{2,1,0:T(8,128)(2,1)S(1)}, u32[]{:S(2)}, u32[]{:S(2)}) %all-to-all-start) | async-done | bytes 262176 | tf_op jit(solution)/shard_map/while/body/eval_jaxpr/all_to_all | solution.py:9
  479.6 4.8 all-to-all-start
  484.4 3.1 gather_fusion
  487.6 16.9 %all-to-all-done = bf16[32,16,256]{2,1,0:T(8,128)(2,1)S(1)} async-done(((bf16[32,16,256]{2,1,0:T(8,128)(2,1)}), bf16[32,16,256]{2,1,0:T(8,128)(2,1)S(1)}, u32[]{:S(2)}, u32[]{:S(2)}) %all-to-all-start) | async-done | bytes 262176 | tf_op jit(solution)/shard_map/while/body/eval_jaxpr/all_to_all | solution.py:9
  511.9 4.8 all-to-all-start
  516.7 3.1 gather_fusion
  519.8 17.9 %all-to-all-done = bf16[32,16,256]{2,1,0:T(8,128)(2,1)S(1)} async-done(((bf16[32,16,256]{2,1,0:T(8,128)(2,1)}), bf16[32,16,256]{2,1,0:T(8,128)(2,1)S(1)}, u32[]{:S(2)}, u32[]{:S(2)}) %all-to-all-start) | async-done | bytes 262176 | tf_op jit(solution)/shard_map/while/body/eval_jaxpr/all_to_all | solution.py:9
  545.1 4.8 all-to-all-start
  549.9 3.1 gather_fusion
  553.1 19.4 %all-to-all-done = bf16[32,16,256]{2,1,0:T(8,128)(2,1)S(1)} async-done(((bf16[32,16,256]{2,1,0:T(8,128)(2,1)}), bf16[32,16,256]{2,1,0:T(8,128)(2,1)S(1)}, u32[]{:S(2)}, u32[]{:S(2)}) %all-to-all-start) | async-done | bytes 262176 | tf_op jit(solution)/shard_map/while/body/eval_jaxpr/all_to_all | solution.py:9
  579.8 4.8 all-to-all-start
  584.6 3.1 gather_fusion
  587.8 17.1 %all-to-all-done = bf16[32,16,256]{2,1,0:T(8,128)(2,1)S(1)} async-done(((bf16[32,16,256]{2,1,0:T(8,128)(2,1)}), bf16[32,16,256]{2,1,0:T(8,128)(2,1)S(1)}, u32[]{:S(2)}, u32[]{:S(2)}) %all-to-all-start) | async-done | bytes 262176 | tf_op jit(solution)/shard_map/while/body/eval_jaxpr/all_to_all | solution.py:9
  612.2 4.7 all-to-all-start
  620.2 17.4 %all-to-all-done = bf16[32,16,256]{2,1,0:T(8,128)(2,1)S(1)} async-done(((bf16[32,16,256]{2,1,0:T(8,128)(2,1)}), bf16[32,16,256]{2,1,0:T(8,128)(2,1)S(1)}, u32[]{:S(2)}, u32[]{:S(2)}) %all-to-all-start) | async-done | bytes 262176 | tf_op jit(solution)/shard_map/while/body/eval_jaxpr/all_to_all | solution.py:9
  (216 shorter events, 119.8 us)
Async XLA Ops:
  0.0 127.5 %copy-start = (s32[1024]{0:T(1024)S(1)}, s32[1024]{0:T(1024)}, u32[]{:S(2)}) copy-start(s32[1024]{0:T(1024)} %param.9) | copy-start | bytes 12292
  1.4 132.3 %all-to-all-start.1 = ((bf16[32,16,256]{2,1,0:T(8,128)(2,1)}), bf16[32,16,256]{2,1,0:T(8,128)(2,1)S(1)}, u32[]{:S(2)}, u32[]{:S(2)}) async-start(bf16[32,16,256]{2,1,0:T(8,128)(2,1)} %broadcast_in_dim.96), calls=%async_computation.1 | async-start | bytes 524288 | tf_op jit(solution)/shard_map/all_to_all | solution.py:9
  127.5 6.2 copy-start.1
  135.4 5.0 collective-permute-start
  141.1 32.4 %all-to-all-start = ((bf16[32,16,256]{2,1,0:T(8,128)(2,1)}), bf16[32,16,256]{2,1,0:T(8,128)(2,1)S(1)}, u32[]{:S(2)}, u32[]{:S(2)}) async-start(bf16[32,16,256]{2,1,0:T(8,128)(2,1)} %broadcast_in_dim.128), calls=%async_computation | async-start | bytes 524288 | tf_op jit(solution)/shard_map/while/body/eval_jaxpr/all_to_all | solution.py:9
  175.0 5.0 collective-permute-start
  180.7 25.3 %all-to-all-start = ((bf16[32,16,256]{2,1,0:T(8,128)(2,1)}), bf16[32,16,256]{2,1,0:T(8,128)(2,1)S(1)}, u32[]{:S(2)}, u32[]{:S(2)}) async-start(bf16[32,16,256]{2,1,0:T(8,128)(2,1)} %broadcast_in_dim.128), calls=%async_computation | async-start | bytes 524288 | tf_op jit(solution)/shard_map/while/body/eval_jaxpr/all_to_all | solution.py:9
  207.7 5.0 collective-permute-start
  213.4 24.9 %all-to-all-start = ((bf16[32,16,256]{2,1,0:T(8,128)(2,1)}), bf16[32,16,256]{2,1,0:T(8,128)(2,1)S(1)}, u32[]{:S(2)}, u32[]{:S(2)}) async-start(bf16[32,16,256]{2,1,0:T(8,128)(2,1)} %broadcast_in_dim.128), calls=%async_computation | async-start | bytes 524288 | tf_op jit(solution)/shard_map/while/body/eval_jaxpr/all_to_all | solution.py:9
  239.9 5.0 collective-permute-start
  245.6 25.8 %all-to-all-start = ((bf16[32,16,256]{2,1,0:T(8,128)(2,1)}), bf16[32,16,256]{2,1,0:T(8,128)(2,1)S(1)}, u32[]{:S(2)}, u32[]{:S(2)}) async-start(bf16[32,16,256]{2,1,0:T(8,128)(2,1)} %broadcast_in_dim.128), calls=%async_computation | async-start | bytes 524288 | tf_op jit(solution)/shard_map/while/body/eval_jaxpr/all_to_all | solution.py:9
  273.0 5.0 collective-permute-start
  278.7 27.3 %all-to-all-start = ((bf16[32,16,256]{2,1,0:T(8,128)(2,1)}), bf16[32,16,256]{2,1,0:T(8,128)(2,1)S(1)}, u32[]{:S(2)}, u32[]{:S(2)}) async-start(bf16[32,16,256]{2,1,0:T(8,128)(2,1)} %broadcast_in_dim.128), calls=%async_computation | async-start | bytes 524288 | tf_op jit(solution)/shard_map/while/body/eval_jaxpr/all_to_all | solution.py:9
  307.7 5.0 collective-permute-start
  313.3 25.3 %all-to-all-start = ((bf16[32,16,256]{2,1,0:T(8,128)(2,1)}), bf16[32,16,256]{2,1,0:T(8,128)(2,1)S(1)}, u32[]{:S(2)}, u32[]{:S(2)}) async-start(bf16[32,16,256]{2,1,0:T(8,128)(2,1)} %broadcast_in_dim.128), calls=%async_computation | async-start | bytes 524288 | tf_op jit(solution)/shard_map/while/body/eval_jaxpr/all_to_all | solution.py:9
  340.3 5.0 collective-permute-start
  346.0 25.4 %all-to-all-start = ((bf16[32,16,256]{2,1,0:T(8,128)(2,1)}), bf16[32,16,256]{2,1,0:T(8,128)(2,1)S(1)}, u32[]{:S(2)}, u32[]{:S(2)}) async-start(bf16[32,16,256]{2,1,0:T(8,128)(2,1)} %broadcast_in_dim.128), calls=%async_computation | async-start | bytes 524288 | tf_op jit(solution)/shard_map/while/body/eval_jaxpr/all_to_all | solution.py:9
  373.0 5.0 collective-permute-start
  378.6 25.8 %all-to-all-start = ((bf16[32,16,256]{2,1,0:T(8,128)(2,1)}), bf16[32,16,256]{2,1,0:T(8,128)(2,1)S(1)}, u32[]{:S(2)}, u32[]{:S(2)}) async-start(bf16[32,16,256]{2,1,0:T(8,128)(2,1)} %broadcast_in_dim.128), calls=%async_computation | async-start | bytes 524288 | tf_op jit(solution)/shard_map/while/body/eval_jaxpr/all_to_all | solution.py:9
  406.1 5.0 collective-permute-start
  411.8 28.1 %all-to-all-start = ((bf16[32,16,256]{2,1,0:T(8,128)(2,1)}), bf16[32,16,256]{2,1,0:T(8,128)(2,1)S(1)}, u32[]{:S(2)}, u32[]{:S(2)}) async-start(bf16[32,16,256]{2,1,0:T(8,128)(2,1)} %broadcast_in_dim.128), calls=%async_computation | async-start | bytes 524288 | tf_op jit(solution)/shard_map/while/body/eval_jaxpr/all_to_all | solution.py:9
  441.5 5.0 collective-permute-start
  447.2 25.2 %all-to-all-start = ((bf16[32,16,256]{2,1,0:T(8,128)(2,1)}), bf16[32,16,256]{2,1,0:T(8,128)(2,1)S(1)}, u32[]{:S(2)}, u32[]{:S(2)}) async-start(bf16[32,16,256]{2,1,0:T(8,128)(2,1)} %broadcast_in_dim.128), calls=%async_computation | async-start | bytes 524288 | tf_op jit(solution)/shard_map/while/body/eval_jaxpr/all_to_all | solution.py:9
  473.9 5.0 collective-permute-start
  479.6 24.9 %all-to-all-start = ((bf16[32,16,256]{2,1,0:T(8,128)(2,1)}), bf16[32,16,256]{2,1,0:T(8,128)(2,1)S(1)}, u32[]{:S(2)}, u32[]{:S(2)}) async-start(bf16[32,16,256]{2,1,0:T(8,128)(2,1)} %broadcast_in_dim.128), calls=%async_computation | async-start | bytes 524288 | tf_op jit(solution)/shard_map/while/body/eval_jaxpr/all_to_all | solution.py:9
  506.2 5.0 collective-permute-start
  511.9 25.9 %all-to-all-start = ((bf16[32,16,256]{2,1,0:T(8,128)(2,1)}), bf16[32,16,256]{2,1,0:T(8,128)(2,1)S(1)}, u32[]{:S(2)}, u32[]{:S(2)}) async-start(bf16[32,16,256]{2,1,0:T(8,128)(2,1)} %broadcast_in_dim.128), calls=%async_computation | async-start | bytes 524288 | tf_op jit(solution)/shard_map/while/body/eval_jaxpr/all_to_all | solution.py:9
  539.4 5.0 collective-permute-start
  545.1 27.4 %all-to-all-start = ((bf16[32,16,256]{2,1,0:T(8,128)(2,1)}), bf16[32,16,256]{2,1,0:T(8,128)(2,1)S(1)}, u32[]{:S(2)}, u32[]{:S(2)}) async-start(bf16[32,16,256]{2,1,0:T(8,128)(2,1)} %broadcast_in_dim.128), calls=%async_computation | async-start | bytes 524288 | tf_op jit(solution)/shard_map/while/body/eval_jaxpr/all_to_all | solution.py:9
  574.1 5.0 collective-permute-start
  579.8 25.1 %all-to-all-start = ((bf16[32,16,256]{2,1,0:T(8,128)(2,1)}), bf16[32,16,256]{2,1,0:T(8,128)(2,1)S(1)}, u32[]{:S(2)}, u32[]{:S(2)}) async-start(bf16[32,16,256]{2,1,0:T(8,128)(2,1)} %broadcast_in_dim.128), calls=%async_computation | async-start | bytes 524288 | tf_op jit(solution)/shard_map/while/body/eval_jaxpr/all_to_all | solution.py:9
  606.5 5.0 collective-permute-start
  612.2 25.4 %all-to-all-start = ((bf16[32,16,256]{2,1,0:T(8,128)(2,1)}), bf16[32,16,256]{2,1,0:T(8,128)(2,1)S(1)}, u32[]{:S(2)}, u32[]{:S(2)}) async-start(bf16[32,16,256]{2,1,0:T(8,128)(2,1)} %broadcast_in_dim.128), calls=%async_computation | async-start | bytes 524288 | tf_op jit(solution)/shard_map/while/body/eval_jaxpr/all_to_all | solution.py:9
where the time goes:
time: 644 us; the launch traced here: 640 us
  waiting for transfers between devices  316 us (49%)
  starting transfers between devices  123 us (19%)
  blocking collectives  104 us (16%)
  local copies, waits for them, and re-layouts  69.5 us (11%)
  other arithmetic  17.1 us (3%)
  matrix products  8.98 us (1%)
    all_to_all x16, waiting for transfers between devices, copy_for_each(): lax.all_to_all(jnp.broadcast_to(value[None], (size, *value.shape)), axis,...  270 us
    unnamed x1, blocking collectives  104 us
    all_to_all x16, starting transfers between devices, copy_for_each(): lax.all_to_all(jnp.broadcast_to(value[None], (size, *value.shape)), axis,...  93.7 us
    gather x16, local copies, waits for them, and re-layouts, absorb(): ids = jnp.take(table, where_at)  50.3 us
    ppermute x15, waiting for transfers between devices, shifted(): lax.ppermute(value, axis, [(i, (i + by) % size) for i in range(size)])  45.5 us
    ppermute x15, starting transfers between devices, shifted(): lax.ppermute(value, axis, [(i, (i + by) % size) for i in range(size)])  28.9 us
    reduce_sum x16, other arithmetic, absorb(): chosen = chosen + jnp.sum(jnp.where(hit, scores, 0.0), axis=1)  15.9 us
  transfers between devices with their start and end apart: 31, of which 30 were waited for; matrix products, arithmetic and copies ran while one was open for 9% of the time, Pallas kernels for 0%

commit v1 on v0

v1 whole, which is shorter than its diff:
```python
import math

import jax
import jax.numpy as jnp
from jax import lax
from jax.experimental import pallas as pl
from jax.experimental.pallas import tpu as pltpu
from jax.sharding import PartitionSpec as P

SCALE = 0.125 * math.log2(math.e)
LN2 = math.log(2.0)
LOW = -1e30
START = -1e20
CHUNK = 256


def absorb_chunk(scores, id_row, base, pos_ref, pid_ref, iota_ref, high_ref, sum_ref, hit_ref):
    users = scores.shape[1]
    for half in range(CHUNK // 128):
        ids = jnp.broadcast_to(id_row[:, half * 128 : (half + 1) * 128], (128, 128)).T
        for group in range(users // 128):
            lanes = pl.ds(group * 128, 128)
            pos = pos_ref[:, lanes] - (base + half * 128)
            pid = pid_ref[:, lanes]
            chosen = hit_ref[:, lanes]
            high = high_ref[:, lanes]
            terms = []
            for k in range(16):
                d = scores[pl.ds(half * 128 + k * 8, 8), lanes]
                chosen = jnp.where(iota_ref[pl.ds(k * 8, 8), :] == pos, d, chosen)
                terms.append(jnp.where(ids[k * 8 : k * 8 + 8] == pid, LOW, d * SCALE))
            tops = terms
            while len(tops) > 1:
                tops = [jnp.maximum(a, b) for a, b in zip(tops[::2], tops[1::2])]
            new_high = jnp.maximum(high, tops[0])
            parts = [jnp.exp2(t - new_high) for t in terms]
            while len(parts) > 1:
                parts = [a + b for a, b in zip(parts[::2], parts[1::2])]
            sum_ref[:, lanes] = sum_ref[:, lanes] * jnp.exp2(high - new_high) + parts[0]
            high_ref[:, lanes] = new_high
            hit_ref[:, lanes] = chosen


def look_up(table, pos):
    low, hi = pos & 255, pos >> 8
    count = pos.shape[1]
    one_hot = jnp.where(lax.broadcasted_iota(jnp.int32, (256, count), 0) == low, 1.0, 0.0).astype(jnp.bfloat16)
    pieces = jnp.concatenate([table & 127, (table >> 7) & 127, table >> 14], axis=0)
    found = jnp.dot(pieces.astype(jnp.float32).astype(jnp.bfloat16), one_hot, preferred_element_type=jnp.float32)
    value = found[:32] + 128.0 * found[32:64] + 16384.0 * found[64:]
    mine = lax.broadcasted_iota(jnp.int32, (32, count), 0) == hi
    return jnp.sum(jnp.where(mine, value, 0.0), axis=0, keepdims=True)


def kernel(users_ref, pos_in, items_ref, table_ref, out_ref, ut_ref, s0, s1, pos_ref, pid_ref, iota_ref, high_ref, sum_ref, hit_ref, idf_ref):
    count = users_ref.shape[0]
    chunks = items_ref.shape[0] // CHUNK
    for i in range(count // 256):
        ut_ref[:, pl.ds(i * 256, 256)] = users_ref[pl.ds(i * 256, 256), :].T
    pos = pos_in[...]
    pos_ref[...] = jnp.broadcast_to(pos, pos_ref.shape)
    pid_ref[...] = jnp.broadcast_to(look_up(table_ref[...], pos), pid_ref.shape)
    idf_ref[...] = table_ref[...].astype(jnp.float32)
    iota_ref[...] = lax.broadcasted_iota(jnp.int32, (128, 128), 0)
    high_ref[...] = jnp.full_like(high_ref, START)
    sum_ref[...] = jnp.zeros_like(sum_ref)
    hit_ref[...] = jnp.zeros_like(hit_ref)

    def score(into, chunk):
        rows = pl.ds(pl.multiple_of(chunk * CHUNK, CHUNK), CHUNK)
        for i in range(count // 256):
            cols = pl.ds(i * 256, 256)
            into[:, cols] = jnp.dot(items_ref[rows, :], ut_ref[:, cols], preferred_element_type=jnp.float32)

    def absorb(scores, chunk):
        absorb_chunk(scores, idf_ref[pl.ds(chunk, 1), :], chunk * CHUNK, pos_ref, pid_ref, iota_ref, high_ref, sum_ref, hit_ref)

    score(s0, 0)

    def step(i, _):
        score(s1, 2 * i + 1)
        absorb(s0, 2 * i)
        score(s0, jnp.minimum(2 * i + 2, chunks - 1))
        absorb(s1, 2 * i + 1)
        return 0

    lax.fori_loop(0, chunks // 2, step, 0)
    chosen = jnp.sum(hit_ref[...], axis=0, keepdims=True)
    own = chosen * SCALE
    high = high_ref[...]
    top = jnp.maximum(jnp.max(high, axis=0, keepdims=True), own)
    total = jnp.sum(sum_ref[...] * jnp.exp2(high - top), axis=0, keepdims=True) + jnp.exp2(own - top)
    out_ref[...] = (top - own) * LN2 + jnp.log(total)


def body(users, positives, items, item_ids):
    table = lax.all_gather(item_ids, ("row", "col"), axis=0, tiled=True)
    pool = lax.all_gather(items, ("row", "col"), axis=0, tiled=True)
    count = users.shape[0]
    vmem = pl.BlockSpec(memory_space=pltpu.VMEM)
    state = pltpu.VMEM((8, count), jnp.float32)
    loss = pl.pallas_call(
        kernel,
        out_shape=jax.ShapeDtypeStruct((1, count), jnp.float32),
        in_specs=[vmem] * 4,
        out_specs=vmem,
        scratch_shapes=[
            pltpu.VMEM((256, count), jnp.bfloat16),
            pltpu.VMEM((CHUNK, count), jnp.float32),
            pltpu.VMEM((CHUNK, count), jnp.float32),
            pltpu.VMEM((8, count), jnp.int32),
            state,
            pltpu.VMEM((128, 128), jnp.int32),
            state,
            state,
            state,
            pltpu.VMEM((32, 256), jnp.float32),
        ],
        compiler_params=pltpu.CompilerParams(vmem_limit_bytes=32 * 1024 * 1024),
    )(users, positives.reshape(1, count), pool, table.reshape(32, 256))
    return loss.reshape(count)


def solution(mesh):
    split = P(("row", "col"))
    wide = P(("row", "col"), None)
    return jax.shard_map(body, mesh=mesh, in_specs=(wide, split, wide, split), out_specs=split, check_vma=False)
```

time: 644 us -> 1480 us (2.30)
  waiting for transfers between devices: 316 us -> 1320 us
  starting transfers between devices: 123 us -> 0.01 us
  local copies, waits for them, and re-layouts: 69.5 us -> 4.8 us
  Pallas kernels: 0 us -> 17.5 us
  other arithmetic: 17.1 us -> 0 us
    all_gather x0 -> x1, waiting for transfers between devices: none -> 1320 us  [body(): pool = lax.all_gather(items, ('row', 'col'), axis=0, tiled=True)]
    all_to_all x16 -> x0, waiting for transfers between devices: 270 us -> none  [copy_for_each(): lax.all_to_all(jnp.broadcast_to(value[None], (size, *value.shape)), axis,...]
    all_to_all x16 -> x0, starting transfers between devices: 93.7 us -> none  [copy_for_each(): lax.all_to_all(jnp.broadcast_to(value[None], (size, *value.shape)), axis,...]
    gather x17 -> x0, local copies, waits for them, and re-layouts: 56.4 us -> none  [the longest x16 50.3 us: absorb(): ids = jnp.take(table, where_at)]
    ppermute x15 -> x0, waiting for transfers between devices: 45.5 us -> none  [shifted(): lax.ppermute(value, axis, [(i, (i + by) % size) for i in range(size)])]
    ppermute x15 -> x0, starting transfers between devices: 28.9 us -> none  [shifted(): lax.ppermute(value, axis, [(i, (i + by) % size) for i in range(size)])]
    pallas_call x0 -> x1, Pallas kernels: none -> 17.5 us  [body(): pl.pallas_call(kernel, out_shape=jax.ShapeDtypeStruct((1, count), jnp.flo...]
    reduce_sum x16 -> x0, other arithmetic: 15.9 us -> none  [absorb(): chosen = chosen + jnp.sum(jnp.where(hit, scores, 0.0), axis=1)]
  transfers between devices with their start and end apart: 31 -> 1, of which waited for: 30 -> 1; matrix products, arithmetic and copies ran while one was open for 9% -> 0% of each run, Pallas kernels for 0% -> 0%
where the time goes in v1:
time: 1480 us; the launch traced here: 1470 us
  waiting for transfers between devices  1320 us (89%)
  blocking collectives  108 us (7%)
  Pallas kernels  17.5 us (1%)
    all_gather x1, waiting for transfers between devices, body(): pool = lax.all_gather(items, ('row', 'col'), axis=0, tiled=True)  1320 us
    unnamed x1, blocking collectives  108 us
  transfers between devices with their start and end apart: 1, of which 1 were waited for; matrix products, arithmetic and copies ran while one was open for 0% of the time, Pallas kernels for 0%

profile of v1, /device:TPU:6, one launch (start us, length us, event | category | flops | bytes accessed | tf_op | source)
XLA Modules:
  0.0 1465.4 jit_solution(7962926237179671272)
XLA Ops:
  6.5 0.0 all-gather.2.cloned.1.call-start
  6.5 0.7 all-gather.2.cloned.1.call-update
  7.3 0.9 dynamic-update-slice
  8.1 108.4 %all-reduce = s32[8192]{0:T(1024)S(1)} all-reduce(s32[8192]{0:T(1024)S(1)} %dynamic-update-slice), channel_id=1, replica_groups=mesh['row'=16,'col'=32] {'row','col'}, use_global_device_ids=true, to_apply=%add | all-reduce | flops 8192 | bytes 65536
  116.6 1320.5 %all-gather.2.cloned.1.call-done.items_ref = bf16[8192,256]{1,0:T(8,128)(2,1)} async-done(((bf16[16,256]{1,0:T(8,128)(2,1)}), bf16[8192,256]{1,0:T(8,128)(2,1)}) %all-gather.2.cloned.1.call-update) | async-done | bytes 4194320 | tf_op jit(solution)/shard_map/all_gather | solution.py:98
  1437.1 0.0 copy-start
  1437.1 2.2 copy-done
  1439.3 0.0 copy-start.1
  1439.3 1.0 copy-done.1
  1440.3 0.0 copy-start.2
  1440.3 0.7 copy-done.2
  1441.0 17.5 %shard_map.46 = f32[1,1024]{1,0:T(1,128)} custom-call(bf16[1024,256]{1,0:T(8,128)(2,1)S(1)} %copy-done.1, s32[1,1024]{1,0:T(1,128)S(1)} %bitcast.2, bf16[8192,256]{1,0:T(8,128)(2,1)S(1)} %copy-done, s32[32,256]{1,0:T(8,128)S(1)} %reshape.10.table_ref), custom_call_target="tpu_custom_call" | custom-call | tf_op jit(solution)/shard_map/pallas_call | solution.py:102
  (2 shorter events, 0.0 us)
Async XLA Ops:
  6.5 1430.6 %all-gather.2.cloned.1.call-start = ((), (), s32[]{:S(2)}) async-start(), calls=%async_computation | async-start | bytes 4202496 | tf_op jit(solution)/shard_map/all_gather | solution.py:98
  1437.1 2.2 copy-start
  1439.3 1.0 copy-start.1
  1440.3 0.7 copy-start.2
Sparse Core Ops, SparseCore 0:
  9.6 1427.4 all-gather.1

commit v2 on v0

v2 whole, which is shorter than its diff:
```python
import math

import jax
import jax.numpy as jnp
from jax import lax
from jax.experimental import pallas as pl
from jax.experimental.pallas import tpu as pltpu
from jax.sharding import PartitionSpec as P

MESH = pl.DeviceIdType.MESH
SCALE = 0.125 * math.log2(math.e)
LN2 = math.log(2.0)
LOW = -1e30
START = -1e20
SMALL = 2.0**-80
LARGE = 2.0**100
LAG = 3
NEAR = (4, 12, 1, 15, 2, 14, 3, 13)
FAR = (8, 9, 7, 10, 6, 11, 5)
PAIRS = ((0,), (1, 15), (2, 14), (3, 13), (4, 12), (5, 11), (6, 10), (7, 9), (8,))
IDS_AT = 5
MASK_AT = 10


def place():
    row, col = lax.axis_index("row"), lax.axis_index("col")
    return (row // 2) % 4, (col % 2) * 2 + row // 8, col // 2, row % 2


def device(x, y, z, c):
    return ((y % 2) * 4 + x) * 2 + c, z * 2 + y // 2


def id_columns(table, core):
    halves = []
    for half in range(2):
        rows = table[pl.ds(core * 16, 16), half, :]
        square = jnp.concatenate([rows, jnp.zeros((112, 128), jnp.float32)], axis=0)
        halves.append(square.T)
    return jnp.concatenate(halves, axis=0)


def fill_ids(into, columns, z_from, x_first):
    rows = columns[pl.ds(pl.multiple_of(z_from * 16, 16), 16), :]
    for block in range(16):
        lane = (block % 4) * 4 + block // 4 if x_first else block
        into[pl.ds(block * 16, 16), :] = jnp.broadcast_to(rows[:, lane : lane + 1], (16, 128))


def look_up(table, low, high):
    count = low.shape[1]
    found = None
    for half in range(2):
        ints = table[:, half, :].astype(jnp.int32)
        pieces = jnp.concatenate([ints & 127, (ints >> 7) & 127, ints >> 14], axis=0)
        pieces = pieces.astype(jnp.float32).astype(jnp.bfloat16)
        lanes = lax.broadcasted_iota(jnp.int32, (128, count), 0) + half * 128
        one_hot = jnp.where(lanes == low, 1.0, 0.0).astype(jnp.bfloat16)
        part = jnp.dot(pieces, one_hot, preferred_element_type=jnp.float32)
        found = part if found is None else found + part
    value = found[:32] + 128.0 * found[32:64] + 16384.0 * found[64:]
    mine = lax.broadcasted_iota(jnp.int32, (32, count), 0) == high
    return jnp.sum(jnp.where(mine, value, 0.0), axis=0, keepdims=True)


def split(pos):
    row, col = pos >> 9, (pos >> 4) & 31
    return (row >> 1) & 3, (col & 1) * 2 + (row >> 3), col >> 1, row & 1, pos & 15


def gather_kernel(
    users_hbm, pos_hbm, items_hbm, ids_hbm,
    stat_ref, table_ref, pool_hbm,
    grid, users, pos, ids_in, ids_z, ids_own, ut, prob, key_ref, pid_ref, iota_ref, hit_ref, acc_ref, cols_ref, idc_ref, mine_ref, theirs_ref,
    lsem, s1, r1, s2, r2, s3, r3, si, ri, st, rt, su, ru, se, re, le, sf, rf,
):
    x, y, z, c = place()

    def at(dx, dy, dz):
        return device((x + dx) % 4, (y + dy) % 4, (z + dz) % 16, c)

    partner = device(x, y, z, 1 - c)

    def send(src, dst, out_sem, in_sem, to):
        return pltpu.make_async_remote_copy(src, dst, out_sem, in_sem, device_id=to, device_id_type=MESH)

    barrier = pltpu.get_barrier_semaphore()
    loads = [
        pltpu.make_async_copy(items_hbm, grid.at[0, y, x], lsem.at[0]),
        pltpu.make_async_copy(ids_hbm, ids_in, lsem.at[1]),
        pltpu.make_async_copy(users_hbm, users.at[c], lsem.at[2]),
        pltpu.make_async_copy(pos_hbm, pos.at[c], lsem.at[3]),
    ]
    for load in loads:
        load.start()
    across = [(dx, dy, dc) for dx in range(4) for dy in range(4) for dc in range(2) if (dx, dy, dc) != (0, 0, 0)]

    def other(dx, dy, dc):
        return device((x + dx) % 4, (y + dy) % 4, z, (c + dc) % 2)

    for s in NEAR:
        pl.semaphore_signal(barrier, inc=1, device_id=at(0, 0, s), device_id_type=MESH)
    for to in across:
        pl.semaphore_signal(barrier, inc=1, device_id=other(*to), device_id_type=MESH)
    iota_ref[...] = lax.broadcasted_iota(jnp.int32, (256, 128), 0)
    hit_ref[...] = jnp.zeros_like(hit_ref)
    acc_ref[...] = jnp.zeros_like(acc_ref)
    for load in loads:
        load.wait()
    spread = jnp.concatenate([ids_in[...]] * 8, axis=1).astype(jnp.float32)
    lane = lax.broadcasted_iota(jnp.int32, (1, 128), 1)
    ids_z[0] = jnp.where(lane // 16 == z % 8, spread, 0.0)
    pl.semaphore_wait(barrier, len(NEAR) + len(across))

    def slot(s):
        return (s, y, x) if s < 8 else (s, x, y)

    def ids_copy(s):
        via = 0 if s in NEAR else (4 if s < 9 else 12)
        return send(ids_z.at[via], ids_z.at[s], si.at[s], ri.at[s], at(0, 0, s - via))

    def stage1(s):
        via = 0 if s in NEAR else (4 if s < 9 else 12)
        src = grid.at[slot(via)]
        return send(src, grid.at[slot(s)], s1.at[s], r1.at[s], at(0, 0, s - via))

    def stage2(s, d):
        block = grid.at[slot(s)]
        return send(block, block, s2.at[s, d], r2.at[s, d], at(d, 0, 0) if s < 8 else at(0, d, 0))

    def stage3(s, d):
        blocks = grid.at[slot(s)[:2]]
        return send(blocks, blocks, s3.at[s, d], r3.at[s, d], at(0, d, 0) if s < 8 else at(d, 0, 0))

    def export(s):
        return send(grid.at[s], pool_hbm.at[c, s], se.at[s], re.at[s], partner)

    def export_here(s):
        return pltpu.make_async_copy(grid.at[s], pool_hbm.at[c, s], le.at[s])

    own_row = c * 16 + y * 4 + x

    def table_copy(n, dx, dy, dc):
        dst = table_ref.at[own_row]
        return send(ids_own, dst, st.at[n], rt.at[n], other(dx, dy, dc))

    swaps = [
        send(users.at[c], users.at[c], su.at[0], ru.at[0], partner),
        send(pos.at[c], pos.at[c], su.at[1], ru.at[1], partner),
    ]
    for s in NEAR:
        ids_copy(s).start()
        stage1(s).start()
    for swap in swaps:
        swap.start()

    def turn_users():
        for swap in swaps:
            swap.wait_recv()
        for half in range(2):
            for i in range(4):
                ut[:, pl.ds(half * 1024 + i * 256, 256)] = users[half, pl.ds(i * 256, 256), :].T
        for half in range(2):
            px, py, pz, pc, pe = split(pos[half])
            s = (z - pz + 16) & 15
            block = jnp.where(s < 8, py * 4 + px, px * 4 + py)
            key_ref[half] = jnp.where(pc == c, s * 256 + block * 16 + pe, -1)

    def share_ids():
        for s in (1, 2, 3, 13, 14, 15) + FAR:
            ids_copy(s).wait_recv()
        rows = ids_z[:, 0, :]
        source = (z - lax.broadcasted_iota(jnp.int32, (16, 128), 0) + 16) & 15
        for half in range(2):
            mine = jnp.sum(jnp.where(source // 8 == half, rows, 0.0), axis=0, keepdims=True)
            ids_own[pl.ds(half, 1), :] = mine
        table_ref[own_row] = ids_own[...]
        for n, to in enumerate(across):
            table_copy(n, *to).start()

    def find_ids():
        for n, to in enumerate(across):
            table_copy(n, *to).wait_recv()
        for half in range(2):
            for g in range(8):
                px, py, pz, pc, pe = split(pos[half, pl.ds(g, 1), :])
                pid_ref[half, pl.ds(g, 1), :] = look_up(table_ref, pz * 16 + pe, pc * 16 + py * 4 + px)
        cols_ref[...] = id_columns(table_ref, c)

    def evaluate(s):
        block = grid[s].reshape(256, 256)
        for tile in range(8):
            d = jnp.dot(block, ut[:, pl.ds(tile * 256, 256)], preferred_element_type=jnp.float32)
            prob[s, :, pl.ds(tile * 256, 256)] = jnp.exp2(d * SCALE)
            for part in range(2):
                g = tile * 2 + part
                want = jnp.broadcast_to(key_ref[g // 8, pl.ds(g % 8, 1), :] - s * 256, (8, 128))
                chosen = hit_ref[:, pl.ds(g * 128, 128)]
                for k in range(32):
                    here = d[k * 8 : k * 8 + 8, part * 128 : part * 128 + 128]
                    chosen = jnp.where(iota_ref[pl.ds(k * 8, 8), :] == want, here, chosen)
                hit_ref[:, pl.ds(g * 128, 128)] = chosen

    def collect(s):
        fill_ids(idc_ref, cols_ref, (z - s + 16) & 15, s >= 8)
        for g in range(16):
            pid = jnp.broadcast_to(pid_ref[g // 8, pl.ds(g % 8, 1), :], (8, 128))
            sums = [acc_ref[:, pl.ds(g * 128, 128)], None, None, None]
            for k in range(32):
                rows = pl.ds(k * 8, 8)
                term = jnp.where(idc_ref[rows, :] == pid, 0.0, prob[s, rows, pl.ds(g * 128, 128)])
                sums[k % 4] = term if sums[k % 4] is None else sums[k % 4] + term
            acc_ref[:, pl.ds(g * 128, 128)] = (sums[0] + sums[1]) + (sums[2] + sums[3])

    done = []
    count = len(PAIRS)
    for t in range(count + 2 * LAG):
        if t < count:
            if t == 3:
                for s in (4, 12):
                    ids_copy(s).wait_recv()
                    stage1(s).wait_recv()
                for s in FAR:
                    ids_copy(s).start()
                    stage1(s).start()
            for s in PAIRS[t]:
                if s not in (0, 4, 12):
                    stage1(s).wait_recv()
                for d in (1, 3, 2):
                    stage2(s, d).start()
        if 0 <= t - LAG < count:
            for s in PAIRS[t - LAG]:
                for d in (1, 3, 2):
                    stage2(s, d).wait_recv()
                for d in (1, 3, 2):
                    stage3(s, d).start()
        if t == 1:
            turn_users()
        if t == IDS_AT:
            share_ids()
        if t == MASK_AT:
            find_ids()
        if t - 2 * LAG >= 0:
            for s in PAIRS[t - 2 * LAG]:
                for d in (1, 3, 2):
                    stage3(s, d).wait_recv()
                export(s).start()
                export_here(s).start()
                evaluate(s)
                done.append(s)
        if t >= MASK_AT:
            for s in done:
                collect(s)
            done = []

    for half in range(2):
        for g in range(8):
            lanes = pl.ds((half * 8 + g) * 128, 128)
            mine_ref[half, 0, pl.ds(g, 1), :] = jnp.sum(acc_ref[:, lanes], axis=0, keepdims=True)
            mine_ref[half, 1, pl.ds(g, 1), :] = jnp.sum(hit_ref[:, lanes], axis=0, keepdims=True)
    last = send(mine_ref.at[1 - c], theirs_ref, sf, rf, partner)
    last.start()
    for swap in swaps:
        swap.wait_send()
    for s in NEAR + FAR:
        ids_copy(s).wait_send()
        stage1(s).wait_send()
    for s in range(16):
        for d in (1, 2, 3):
            stage2(s, d).wait_send()
            stage3(s, d).wait_send()
        export(s).wait()
        export_here(s).wait()
    for n, to in enumerate(across):
        table_copy(n, *to).wait_send()
    last.wait()
    chosen = mine_ref[c, 1] + theirs_ref[1]
    total = mine_ref[c, 0] + theirs_ref[0] + jnp.exp2(chosen * SCALE)
    stat_ref[0] = jnp.log(total) - 0.125 * chosen
    stat_ref[1] = total
    stat_ref[2] = chosen
    stat_ref[3] = pid_ref[c]


def finish_kernel(stat_ref, table_hbm, users_hbm, pool_hbm, out_ref, table, users, ut, block, cols, idc, high_ref, sum_ref, sem):
    total = stat_ref[1]
    out_ref[...] = stat_ref[0]
    fine = jnp.where((total > SMALL) & (total < LARGE), 0.0, 1.0)

    @pl.when(jnp.max(fine) > 0.0)
    def _():
        z = lax.axis_index("col") // 2
        for src, dst in ((table_hbm, table), (users_hbm, users)):
            copy = pltpu.make_async_copy(src, dst, sem)
            copy.start()
            copy.wait()
        for i in range(4):
            ut[:, pl.ds(i * 256, 256)] = users[pl.ds(i * 256, 256), :].T
        high_ref[...] = jnp.full_like(high_ref, START)
        sum_ref[...] = jnp.zeros_like(sum_ref)
        for core in range(2):
            cols[...] = id_columns(table, core)

            def absorb(s, x_first):
                copy = pltpu.make_async_copy(pool_hbm.at[core, s], block, sem)
                copy.start()
                copy.wait()
                fill_ids(idc, cols, (z - s + 16) & 15, x_first)
                for g in range(8):
                    lanes = pl.ds(g * 128, 128)
                    d = jnp.dot(block[...].reshape(256, 256), ut[:, lanes], preferred_element_type=jnp.float32)
                    masked = jnp.where(idc[...] == stat_ref[3, pl.ds(g, 1), :], LOW, d * SCALE)
                    high = high_ref[pl.ds(g, 1), :]
                    top = jnp.maximum(high, jnp.max(masked, axis=0, keepdims=True))
                    part = jnp.sum(jnp.exp2(masked - top), axis=0, keepdims=True)
                    sum_ref[pl.ds(g, 1), :] = sum_ref[pl.ds(g, 1), :] * jnp.exp2(high - top) + part
                    high_ref[pl.ds(g, 1), :] = top

            lax.fori_loop(0, 8, lambda s, _: (absorb(s, False), 0)[1], 0)
            lax.fori_loop(8, 16, lambda s, _: (absorb(s, True), 0)[1], 0)
        own = stat_ref[2] * SCALE
        high = high_ref[...]
        top = jnp.maximum(high, own)
        both = sum_ref[...] * jnp.exp2(high - top) + jnp.exp2(own - top)
        out_ref[...] = (top - own) * LN2 + jnp.log(both)


def body(users, positives, items, item_ids):
    hbm = pl.BlockSpec(memory_space=pltpu.HBM)
    vmem = pl.BlockSpec(memory_space=pltpu.VMEM)
    f32, bf16, i32 = jnp.float32, jnp.bfloat16, jnp.int32
    dma = pltpu.SemaphoreType.DMA
    stat, table, pool = pl.pallas_call(
        gather_kernel,
        name="gather_scores",
        out_shape=(
            jax.ShapeDtypeStruct((4, 8, 128), f32),
            jax.ShapeDtypeStruct((32, 2, 128), f32),
            jax.ShapeDtypeStruct((2, 16, 4, 4, 16, 256), bf16),
        ),
        in_specs=[hbm] * 4,
        out_specs=(vmem, vmem, hbm),
        scratch_shapes=[
            pltpu.VMEM((16, 4, 4, 16, 256), bf16),
            pltpu.VMEM((2, 1024, 256), bf16),
            pltpu.VMEM((2, 8, 128), i32),
            pltpu.VMEM((1, 16), i32),
            pltpu.VMEM((16, 1, 128), f32),
            pltpu.VMEM((2, 128), f32),
            pltpu.VMEM((256, 2048), bf16),
            pltpu.VMEM((16, 256, 2048), f32),
            pltpu.VMEM((2, 8, 128), i32),
            pltpu.VMEM((2, 8, 128), f32),
            pltpu.VMEM((256, 128), i32),
            pltpu.VMEM((8, 2048), f32),
            pltpu.VMEM((8, 2048), f32),
            pltpu.VMEM((256, 128), f32),
            pltpu.VMEM((256, 128), f32),
            pltpu.VMEM((2, 2, 8, 128), f32),
            pltpu.VMEM((2, 8, 128), f32),
            dma((4,)),
            dma((16,)), dma((16,)),
            dma((16, 4)), dma((16, 4)),
            dma((16, 4)), dma((16, 4)),
            dma((16,)), dma((16,)),
            dma((31,)), dma((31,)),
            dma((2,)), dma((2,)),
            dma((16,)), dma((16,)), dma((16,)),
            dma, dma,
        ],
        compiler_params=pltpu.CompilerParams(collective_id=0, has_side_effects=True, vmem_limit_bytes=67_000_000),
    )(users, positives.reshape(8, 128), items, item_ids.reshape(1, 16))
    loss = pl.pallas_call(
        finish_kernel,
        name="finish",
        out_shape=jax.ShapeDtypeStruct((8, 128), f32),
        in_specs=[vmem, hbm, hbm, hbm],
        out_specs=vmem,
        scratch_shapes=[
            pltpu.VMEM((32, 2, 128), f32),
            pltpu.VMEM((1024, 256), bf16),
            pltpu.VMEM((256, 1024), bf16),
            pltpu.VMEM((4, 4, 16, 256), bf16),
            pltpu.VMEM((256, 128), f32),
            pltpu.VMEM((256, 128), f32),
            pltpu.VMEM((8, 128), f32),
            pltpu.VMEM((8, 128), f32),
            dma,
        ],
        compiler_params=pltpu.CompilerParams(vmem_limit_bytes=67_000_000),
    )(stat, table, users, pool)
    return loss.reshape(1024)


def solution(mesh):
    split_all = P(("row", "col"))
    wide = P(("row", "col"), None)
    return jax.shard_map(body, mesh=mesh, in_specs=(wide, split_all, wide, split_all), out_specs=split_all, check_vma=False)
```

time: 644 us -> 97.2 us (0.15)
  waiting for transfers between devices: 316 us -> 0 us
  starting transfers between devices: 123 us -> 0 us
  blocking collectives: 104 us -> 0 us
  Pallas kernels: 0 us -> 95.2 us
  local copies, waits for them, and re-layouts: 69.5 us -> 0 us
  other arithmetic: 17.1 us -> 0 us
  matrix products: 8.98 us -> 0 us
    all_to_all x16 -> x0, waiting for transfers between devices: 270 us -> none  [copy_for_each(): lax.all_to_all(jnp.broadcast_to(value[None], (size, *value.shape)), axis,...]
    unnamed x1 -> x0, blocking collectives: 104 us -> none
    pallas_call x0 -> x2, Pallas kernels: none -> 95.2 us  [the longest x1 49.5 us: body(): pl.pallas_call(finish_kernel, name='finish', out_shape=jax.ShapeDtypeStru...]
    all_to_all x16 -> x0, starting transfers between devices: 93.7 us -> none  [copy_for_each(): lax.all_to_all(jnp.broadcast_to(value[None], (size, *value.shape)), axis,...]
    gather x17 -> x0, local copies, waits for them, and re-layouts: 56.4 us -> none  [the longest x16 50.3 us: absorb(): ids = jnp.take(table, where_at)]
    ppermute x15 -> x0, waiting for transfers between devices: 45.5 us -> none  [shifted(): lax.ppermute(value, axis, [(i, (i + by) % size) for i in range(size)])]
    ppermute x15 -> x0, starting transfers between devices: 28.9 us -> none  [shifted(): lax.ppermute(value, axis, [(i, (i + by) % size) for i in range(size)])]
    reduce_sum x16 -> x0, other arithmetic: 15.9 us -> none  [absorb(): chosen = chosen + jnp.sum(jnp.where(hit, scores, 0.0), axis=1)]
  transfers between devices with their start and end apart: 31 -> 0, of which waited for: 30 -> 0; matrix products, arithmetic and copies ran while one was open for 9% -> 0% of each run, Pallas kernels for 0% -> 0%
where the time goes in v2:
time: 97.2 us; the launch traced here: 95.4 us
  Pallas kernels  95.2 us (98%)
    pallas_call x1, Pallas kernels, body(): pl.pallas_call(finish_kernel, name='finish', out_shape=jax.ShapeDtypeStru...  49.5 us
    pallas_call x1, Pallas kernels, body(): pl.pallas_call(gather_kernel, name='gather_scores', out_shape=(jax.ShapeD...  45.8 us

profile of v2, /device:TPU:6, one launch (start us, length us, event | category | flops | bytes accessed | tf_op | source)
XLA Modules:
  0.0 95.4 jit_solution(1170551003882753596)
XLA Ops:
  0.0 45.8 %gather_scores.1 = (f32[4,8,128]{2,1,0:T(8,128)}, f32[32,2,128]{2,1,0:T(2,128)}, bf16[2,16,4,4,16,256]{5,4,3,2,1,0:T(8,128)(2,1)}) custom-call(bf16[1024,256]{1,0:T(8,128)(2,1)} %users_hbm.3, s32[8,128]{1,0:T(8,128)} %bitcast.3, bf16[16,256]{1,0:T(8,128)(2,1)} %items_hbm.1, s32[1,16]{1,0:T(1,128)} %bitcast.4), custom_call_target="tpu_custom_call" | custom-call | tf_op jit(solution)/shard_map/gather_scores/pallas_call | solution.py:333
  45.8 49.5 %finish.1 = f32[8,128]{1,0:T(8,128)} custom-call(f32[4,8,128]{2,1,0:T(8,128)} %get-tuple-element.8.stat_ref, f32[32,2,128]{2,1,0:T(2,128)} %get-tuple-element.9.table_hbm, bf16[1024,256]{1,0:T(8,128)(2,1)} %users_hbm.3, bf16[2,16,4,4,16,256]{5,4,3,2,1,0:T(8,128)(2,1)} %get-tuple-element.10.pool_hbm), custom_call_target="tpu_custom_call" | custom-call | tf_op jit(solution)/shard_map/finish/pallas_call | solution.py:373

commit v3 on v2

--- a/solution.py
+++ b/solution.py
@@ -14,12 +14,10 @@
 START = -1e20
 SMALL = 2.0**-80
 LARGE = 2.0**100
-LAG = 3
-NEAR = (4, 12, 1, 15, 2, 14, 3, 13)
+IDS_NEAR = (4, 12, 1, 15, 2, 14, 3, 13)
+NEAR = (4, 12, 3, 13)
 FAR = (8, 9, 7, 10, 6, 11, 5)
-PAIRS = ((0,), (1, 15), (2, 14), (3, 13), (4, 12), (5, 11), (6, 10), (7, 9), (8,))
-IDS_AT = 5
-MASK_AT = 10
+WHOLE = (1, 15, 2, 14)
 
 
 def place():
@@ -31,20 +29,27 @@
     return ((y % 2) * 4 + x) * 2 + c, z * 2 + y // 2
 
 
-def id_columns(table, core):
+def id_columns(table, core, x_first):
     halves = []
     for half in range(2):
-        rows = table[pl.ds(core * 16, 16), half, :]
+        if x_first:
+            picks = [table[core * 16 + (n % 4) * 4 + n // 4, pl.ds(half, 1), :] for n in range(16)]
+            rows = jnp.concatenate(picks, axis=0)
+        else:
+            rows = table[pl.ds(core * 16, 16), half, :]
         square = jnp.concatenate([rows, jnp.zeros((112, 128), jnp.float32)], axis=0)
         halves.append(square.T)
     return jnp.concatenate(halves, axis=0)
 
 
-def fill_ids(into, columns, z_from, x_first):
-    rows = columns[pl.ds(pl.multiple_of(z_from * 16, 16), 16), :]
+def turned(s):
+    return jnp.where((s >= 8) & (s < 14), 1, 0)
+
+
+def fill_ids(into, columns, z_from, order):
+    rows = columns[order, pl.ds(pl.multiple_of(z_from * 16, 16), 16), :]
     for block in range(16):
-        lane = (block % 4) * 4 + block // 4 if x_first else block
-        into[pl.ds(block * 16, 16), :] = jnp.broadcast_to(rows[:, lane : lane + 1], (16, 128))
+        into[pl.ds(block * 16, 16), :] = jnp.broadcast_to(rows[:, block : block + 1], (16, 128))
 
 
 def look_up(table, low, high):
@@ -72,7 +77,7 @@
     users_hbm, pos_hbm, items_hbm, ids_hbm,
     stat_ref, table_ref, pool_hbm,
     grid, users, pos, ids_in, ids_z, ids_own, ut, prob, key_ref, pid_ref, iota_ref, hit_ref, acc_ref, cols_ref, idc_ref, mine_ref, theirs_ref,
-    lsem, s1, r1, s2, r2, s3, r3, si, ri, st, rt, su, ru, se, re, le, sf, rf,
+    lsem, s1, r1, s2, r2, s3, r3, sw, rw, si, ri, st, rt, su, ru, se, re, le, sf, rf,
 ):
     x, y, z, c = place()
 
@@ -98,7 +103,7 @@
     def other(dx, dy, dc):
         return device((x + dx) % 4, (y + dy) % 4, z, (c + dc) % 2)
 
-    for s in NEAR:
+    for s in IDS_NEAR:
         pl.semaphore_signal(barrier, inc=1, device_id=at(0, 0, s), device_id_type=MESH)
     for to in across:
         pl.semaphore_signal(barrier, inc=1, device_id=other(*to), device_id_type=MESH)
@@ -110,13 +115,13 @@
     spread = jnp.concatenate([ids_in[...]] * 8, axis=1).astype(jnp.float32)
     lane = lax.broadcasted_iota(jnp.int32, (1, 128), 1)
     ids_z[0] = jnp.where(lane // 16 == z % 8, spread, 0.0)
-    pl.semaphore_wait(barrier, len(NEAR) + len(across))
+    pl.semaphore_wait(barrier, len(IDS_NEAR) + len(across))
 
     def slot(s):
-        return (s, y, x) if s < 8 else (s, x, y)
+        return (s, x, y) if 8 <= s < 14 else (s, y, x)
 
     def ids_copy(s):
-        via = 0 if s in NEAR else (4 if s < 9 else 12)
+        via = 0 if s in IDS_NEAR else (4 if s < 9 else 12)
         return send(ids_z.at[via], ids_z.at[s], si.at[s], ri.at[s], at(0, 0, s - via))
 
     def stage1(s):
@@ -131,6 +136,9 @@
     def stage3(s, d):
         blocks = grid.at[slot(s)[:2]]
         return send(blocks, blocks, s3.at[s, d], r3.at[s, d], at(0, d, 0) if s < 8 else at(d, 0, 0))
+
+    def whole(s):
+        return send(grid.at[0], grid.at[s], sw.at[s], rw.at[s], at(0, 0, s))
 
     def export(s):
         return send(grid.at[s], pool_hbm.at[c, s], se.at[s], re.at[s], partner)
@@ -149,8 +157,11 @@
         send(pos.at[c], pos.at[c], su.at[1], ru.at[1], partner),
     ]
     for s in NEAR:
+        stage1(s).start()
+    for d in (1, 3, 2):
+        stage2(0, d).start()
+    for s in IDS_NEAR:
         ids_copy(s).start()
-        stage1(s).start()
     for swap in swaps:
         swap.start()
 
@@ -163,7 +174,7 @@
         for half in range(2):
             px, py, pz, pc, pe = split(pos[half])
             s = (z - pz + 16) & 15
-            block = jnp.where(s < 8, py * 4 + px, px * 4 + py)
+            block = jnp.where(turned(s) == 0, py * 4 + px, px * 4 + py)
             key_ref[half] = jnp.where(pc == c, s * 256 + block * 16 + pe, -1)
 
     def share_ids():
@@ -185,7 +196,8 @@
             for g in range(8):
                 px, py, pz, pc, pe = split(pos[half, pl.ds(g, 1), :])
                 pid_ref[half, pl.ds(g, 1), :] = look_up(table_ref, pz * 16 + pe, pc * 16 + py * 4 + px)
-        cols_ref[...] = id_columns(table_ref, c)
+        for order in range(2):
+            cols_ref[order] = id_columns(table_ref, c, order == 1)
 
     def evaluate(s):
         block = grid[s].reshape(256, 256)
@@ -202,7 +214,7 @@
                 hit_ref[:, pl.ds(g * 128, 128)] = chosen
 
     def collect(s):
-        fill_ids(idc_ref, cols_ref, (z - s + 16) & 15, s >= 8)
+        fill_ids(idc_ref, cols_ref, (z - s + 16) & 15, turned(s))
         for g in range(16):
             pid = jnp.broadcast_to(pid_ref[g // 8, pl.ds(g % 8, 1), :], (8, 128))
             sums = [acc_ref[:, pl.ds(g * 128, 128)], None, None, None]
@@ -212,46 +224,77 @@
                 sums[k % 4] = term if sums[k % 4] is None else sums[k % 4] + term
             acc_ref[:, pl.ds(g * 128, 128)] = (sums[0] + sums[1]) + (sums[2] + sums[3])
 
-    done = []
-    count = len(PAIRS)
-    for t in range(count + 2 * LAG):
-        if t < count:
-            if t == 3:
-                for s in (4, 12):
-                    ids_copy(s).wait_recv()
-                    stage1(s).wait_recv()
-                for s in FAR:
-                    ids_copy(s).start()
-                    stage1(s).start()
-            for s in PAIRS[t]:
-                if s not in (0, 4, 12):
-                    stage1(s).wait_recv()
-                for d in (1, 3, 2):
-                    stage2(s, d).start()
-        if 0 <= t - LAG < count:
-            for s in PAIRS[t - LAG]:
-                for d in (1, 3, 2):
-                    stage2(s, d).wait_recv()
-                for d in (1, 3, 2):
-                    stage3(s, d).start()
-        if t == 1:
-            turn_users()
-        if t == IDS_AT:
-            share_ids()
-        if t == MASK_AT:
-            find_ids()
-        if t - 2 * LAG >= 0:
-            for s in PAIRS[t - 2 * LAG]:
-                for d in (1, 3, 2):
-                    stage3(s, d).wait_recv()
-                export(s).start()
-                export_here(s).start()
-                evaluate(s)
-                done.append(s)
-        if t >= MASK_AT:
-            for s in done:
-                collect(s)
-            done = []
+    def forward(slots):
+        for s in slots:
+            for d in (1, 3, 2):
+                stage2(s, d).wait_recv()
+            for d in (1, 3, 2):
+                stage3(s, d).start()
+
+    def landed(s):
+        for d in (1, 3, 2):
+            send(grid.at[s, 0], grid.at[s, 0], s3.at[s, d], r3.at[s, d], partner).wait_recv()
+
+    def hand_on(s):
+        export(s).start()
+        export_here(s).start()
+
+    def loop(count, slot_of, step):
+        def turn(i, carry):
+            step(slot_of(i))
+            return carry
+
+        lax.fori_loop(0, count, turn, 0)
+
+    def early(s):
+        landed(s)
+        hand_on(s)
+        evaluate(s)
+
+    def late_whole(s):
+        send(grid.at[s], grid.at[s], sw.at[s], rw.at[s], partner).wait_recv()
+        hand_on(s)
+        evaluate(s)
+        collect(s)
+
+    def late(s):
+        early(s)
+        collect(s)
+
+    turn_users()
+    forward((0,))
+    for s in (4, 12):
+        stage1(s).wait_recv()
+        ids_copy(s).wait_recv()
+    for s in FAR:
+        ids_copy(s).start()
+        stage1(s).start()
+    for s in (4, 12):
+        for d in (1, 3, 2):
+            stage2(s, d).start()
+    for s in (3, 13):
+        stage1(s).wait_recv()
+        for d in (1, 3, 2):
+            stage2(s, d).start()
+    landed(0)
+    for s in WHOLE:
+        whole(s).start()
+    hand_on(0)
+    evaluate(0)
+    forward((4, 12, 3, 13))
+    share_ids()
+    for s in FAR:
+        stage1(s).wait_recv()
+        for d in (1, 3, 2):
+            stage2(s, d).start()
+    loop(2, lambda i: 4 + 8 * i, early)
+    forward(FAR[:4])
+    loop(2, lambda i: 3 + 10 * i, early)
+    forward(FAR[4:])
+    find_ids()
+    loop(5, lambda i: jnp.where(i < 2, i * 4, jnp.where(i == 2, 12, 10 * i - 27)), collect)
+    loop(4, lambda i: jnp.where(i % 2 == 0, 1 + i // 2, 15 - i // 2), late_whole)
+    loop(7, lambda i: 8 + jnp.where(i % 2 == 1, (i + 1) // 2, -(i // 2)), late)
 
     for half in range(2):
         for g in range(8):
@@ -262,21 +305,27 @@
     last.start()
     for swap in swaps:
         swap.wait_send()
+    for s in range(1, 16):
+        ids_copy(s).wait_send()
+    for s in WHOLE:
+        whole(s).wait_send()
     for s in NEAR + FAR:
-        ids_copy(s).wait_send()
         stage1(s).wait_send()
-    for s in range(16):
+    for s in (0,) + NEAR + FAR:
         for d in (1, 2, 3):
             stage2(s, d).wait_send()
             stage3(s, d).wait_send()
+    for s in range(16):
         export(s).wait()
         export_here(s).wait()
     for n, to in enumerate(across):
         table_copy(n, *to).wait_send()
     last.wait()
     chosen = mine_ref[c, 1] + theirs_ref[1]
-    total = mine_ref[c, 0] + theirs_ref[0] + jnp.exp2(chosen * SCALE)
-    stat_ref[0] = jnp.log(total) - 0.125 * chosen
+    others = mine_ref[c, 0] + theirs_ref[0]
+    own = jnp.exp2(chosen * SCALE)
+    total = others + own
+    stat_ref[0] = jnp.where(others < own, jnp.log(1.0 + others / own), jnp.log(total) - 0.125 * chosen)
     stat_ref[1] = total
     stat_ref[2] = chosen
     stat_ref[3] = pid_ref[c]
@@ -299,13 +348,14 @@
         high_ref[...] = jnp.full_like(high_ref, START)
         sum_ref[...] = jnp.zeros_like(sum_ref)
         for core in range(2):
-            cols[...] = id_columns(table, core)
-
-            def absorb(s, x_first):
+            for order in range(2):
+                cols[order] = id_columns(table, core, order == 1)
+
+            def absorb(s, _):
                 copy = pltpu.make_async_copy(pool_hbm.at[core, s], block, sem)
                 copy.start()
                 copy.wait()
-                fill_ids(idc, cols, (z - s + 16) & 15, x_first)
+                fill_ids(idc, cols, (z - s + 16) & 15, turned(s))
                 for g in range(8):
                     lanes = pl.ds(g * 128, 128)
                     d = jnp.dot(block[...].reshape(256, 256), ut[:, lanes], preferred_element_type=jnp.float32)
@@ -316,8 +366,9 @@
                     sum_ref[pl.ds(g, 1), :] = sum_ref[pl.ds(g, 1), :] * jnp.exp2(high - top) + part
                     high_ref[pl.ds(g, 1), :] = top
 
-            lax.fori_loop(0, 8, lambda s, _: (absorb(s, False), 0)[1], 0)
-            lax.fori_loop(8, 16, lambda s, _: (absorb(s, True), 0)[1], 0)
+                return 0
+
+            lax.fori_loop(0, 16, absorb, 0)
         own = stat_ref[2] * SCALE
         high = high_ref[...]
         top = jnp.maximum(high, own)
@@ -354,7 +405,7 @@
             pltpu.VMEM((256, 128), i32),
             pltpu.VMEM((8, 2048), f32),
             pltpu.VMEM((8, 2048), f32),
-            pltpu.VMEM((256, 128), f32),
+            pltpu.VMEM((2, 256, 128), f32),
             pltpu.VMEM((256, 128), f32),
             pltpu.VMEM((2, 2, 8, 128), f32),
             pltpu.VMEM((2, 8, 128), f32),
@@ -362,6 +413,7 @@
             dma((16,)), dma((16,)),
             dma((16, 4)), dma((16, 4)),
             dma((16, 4)), dma((16, 4)),
+            dma((16,)), dma((16,)),
             dma((16,)), dma((16,)),
             dma((31,)), dma((31,)),
             dma((2,)), dma((2,)),
@@ -381,7 +433,7 @@
             pltpu.VMEM((1024, 256), bf16),
             pltpu.VMEM((256, 1024), bf16),
             pltpu.VMEM((4, 4, 16, 256), bf16),
-            pltpu.VMEM((256, 128), f32),
+            pltpu.VMEM((2, 256, 128), f32),
             pltpu.VMEM((256, 128), f32),
             pltpu.VMEM((8, 128), f32),
             pltpu.VMEM((8, 128), f32),

time: 97.2 us -> 96.5 us (level)
  no operation moved by 1% of the time
where the time goes in v3:
time: 96.5 us; the launch traced here: 95.6 us
  Pallas kernels  95.6 us (99%)
    pallas_call x1, Pallas kernels, body(): pl.pallas_call(finish_kernel, name='finish', out_shape=jax.ShapeDtypeStru...  49.5 us
    pallas_call x1, Pallas kernels, body(): pl.pallas_call(gather_kernel, name='gather_scores', out_shape=(jax.ShapeD...  46.1 us

profile of v3, /device:TPU:6, one launch (start us, length us, event | category | flops | bytes accessed | tf_op | source)
XLA Modules:
  0.0 95.6 jit_solution(2141257747208887942)
XLA Ops:
  0.0 46.1 %gather_scores.1 = (f32[4,8,128]{2,1,0:T(8,128)}, f32[32,2,128]{2,1,0:T(2,128)}, bf16[2,16,4,4,16,256]{5,4,3,2,1,0:T(8,128)(2,1)}) custom-call(bf16[1024,256]{1,0:T(8,128)(2,1)} %users_hbm.3, s32[8,128]{1,0:T(8,128)} %bitcast.3, bf16[16,256]{1,0:T(8,128)(2,1)} %items_hbm.1, s32[1,16]{1,0:T(1,128)} %bitcast.4), custom_call_target="tpu_custom_call" | custom-call | tf_op jit(solution)/shard_map/gather_scores/pallas_call | solution.py:384
  46.1 49.5 %finish.1 = f32[8,128]{1,0:T(8,128)} custom-call(f32[4,8,128]{2,1,0:T(8,128)} %get-tuple-element.8.stat_ref, f32[32,2,128]{2,1,0:T(2,128)} %get-tuple-element.9.table_hbm, bf16[1024,256]{1,0:T(8,128)(2,1)} %users_hbm.3, bf16[2,16,4,4,16,256]{5,4,3,2,1,0:T(8,128)(2,1)} %get-tuple-element.10.pool_hbm), custom_call_target="tpu_custom_call" | custom-call | tf_op jit(solution)/shard_map/finish/pallas_call | solution.py:425

commit v4 on v3

--- a/solution.py
+++ b/solution.py
@@ -14,9 +14,8 @@
 START = -1e20
 SMALL = 2.0**-80
 LARGE = 2.0**100
-IDS_NEAR = (4, 12, 1, 15, 2, 14, 3, 13)
-NEAR = (4, 12, 3, 13)
-FAR = (8, 9, 7, 10, 6, 11, 5)
+NEAR = (4, 12, 6, 10, 5, 11, 3, 13)
+FAR = (8, 9, 7)
 WHOLE = (1, 15, 2, 14)
 
 
@@ -103,65 +102,75 @@
     def other(dx, dy, dc):
         return device((x + dx) % 4, (y + dy) % 4, z, (c + dc) % 2)
 
-    for s in IDS_NEAR:
+    for s in NEAR + WHOLE:
         pl.semaphore_signal(barrier, inc=1, device_id=at(0, 0, s), device_id_type=MESH)
     for to in across:
         pl.semaphore_signal(barrier, inc=1, device_id=other(*to), device_id_type=MESH)
     iota_ref[...] = lax.broadcasted_iota(jnp.int32, (256, 128), 0)
     hit_ref[...] = jnp.zeros_like(hit_ref)
     acc_ref[...] = jnp.zeros_like(acc_ref)
-    for load in loads:
+    for load in loads[:2]:
         load.wait()
     spread = jnp.concatenate([ids_in[...]] * 8, axis=1).astype(jnp.float32)
     lane = lax.broadcasted_iota(jnp.int32, (1, 128), 1)
     ids_z[0] = jnp.where(lane // 16 == z % 8, spread, 0.0)
-    pl.semaphore_wait(barrier, len(IDS_NEAR) + len(across))
+    pl.semaphore_wait(barrier, len(NEAR) + len(WHOLE) + len(across))
 
     def slot(s):
         return (s, x, y) if 8 <= s < 14 else (s, y, x)
 
+    def via(s):
+        return 0 if s not in FAR else (12 if s == 9 else 4)
+
     def ids_copy(s):
-        via = 0 if s in IDS_NEAR else (4 if s < 9 else 12)
-        return send(ids_z.at[via], ids_z.at[s], si.at[s], ri.at[s], at(0, 0, s - via))
+        mark = 0 if s == 4 else (1 if s == 12 else 2)
+        return send(ids_z.at[via(s)], ids_z.at[s], si, ri.at[mark], at(0, 0, s - via(s)))
 
     def stage1(s):
-        via = 0 if s in NEAR else (4 if s < 9 else 12)
-        src = grid.at[slot(via)]
-        return send(src, grid.at[slot(s)], s1.at[s], r1.at[s], at(0, 0, s - via))
+        return send(grid.at[slot(via(s))], grid.at[slot(s)], s1, r1.at[s], at(0, 0, s - via(s)))
 
     def stage2(s, d):
         block = grid.at[slot(s)]
-        return send(block, block, s2.at[s, d], r2.at[s, d], at(d, 0, 0) if s < 8 else at(0, d, 0))
+        return send(block, block, s2, r2.at[s], at(d, 0, 0) if s < 8 else at(0, d, 0))
 
     def stage3(s, d):
         blocks = grid.at[slot(s)[:2]]
-        return send(blocks, blocks, s3.at[s, d], r3.at[s, d], at(0, d, 0) if s < 8 else at(d, 0, 0))
+        return send(blocks, blocks, s3, r3.at[s], at(0, d, 0) if s < 8 else at(d, 0, 0))
+
+    def mark_whole(s):
+        return jnp.where(s < 8, s - 1, 17 - s)
+
+    def sized(ref, out_sem, in_sem):
+        return send(ref, ref, out_sem, in_sem, partner)
 
     def whole(s):
-        return send(grid.at[0], grid.at[s], sw.at[s], rw.at[s], at(0, 0, s))
+        return send(grid.at[0], grid.at[s], sw, rw.at[mark_whole(s)], at(0, 0, s))
 
     def export(s):
-        return send(grid.at[s], pool_hbm.at[c, s], se.at[s], re.at[s], partner)
+        return send(grid.at[s], pool_hbm.at[c, s], se, re, partner)
 
     def export_here(s):
-        return pltpu.make_async_copy(grid.at[s], pool_hbm.at[c, s], le.at[s])
+        return pltpu.make_async_copy(grid.at[s], pool_hbm.at[c, s], le)
 
     own_row = c * 16 + y * 4 + x
 
-    def table_copy(n, dx, dy, dc):
+    def table_copy(dx, dy, dc):
         dst = table_ref.at[own_row]
-        return send(ids_own, dst, st.at[n], rt.at[n], other(dx, dy, dc))
+        return send(ids_own, dst, st, rt, other(dx, dy, dc))
 
     swaps = [
         send(users.at[c], users.at[c], su.at[0], ru.at[0], partner),
         send(pos.at[c], pos.at[c], su.at[1], ru.at[1], partner),
     ]
     for s in NEAR:
+        ids_copy(s).start()
         stage1(s).start()
+    for s in WHOLE:
+        ids_copy(s).start()
     for d in (1, 3, 2):
         stage2(0, d).start()
-    for s in IDS_NEAR:
-        ids_copy(s).start()
+    for load in loads[2:]:
+        load.wait()
     for swap in swaps:
         swap.start()
 
@@ -178,20 +187,18 @@
             key_ref[half] = jnp.where(pc == c, s * 256 + block * 16 + pe, -1)
 
     def share_ids():
-        for s in (1, 2, 3, 13, 14, 15) + FAR:
-            ids_copy(s).wait_recv()
+        sized(ids_z.at[pl.ds(0, 13)], si, ri.at[2]).wait_recv()
         rows = ids_z[:, 0, :]
         source = (z - lax.broadcasted_iota(jnp.int32, (16, 128), 0) + 16) & 15
         for half in range(2):
             mine = jnp.sum(jnp.where(source // 8 == half, rows, 0.0), axis=0, keepdims=True)
             ids_own[pl.ds(half, 1), :] = mine
         table_ref[own_row] = ids_own[...]
-        for n, to in enumerate(across):
-            table_copy(n, *to).start()
+        for to in across:
+            table_copy(*to).start()
 
     def find_ids():
-        for n, to in enumerate(across):
-            table_copy(n, *to).wait_recv()
+        sized(table_ref.at[pl.ds(0, 31)], st, rt).wait_recv()
         for half in range(2):
             for g in range(8):
                 px, py, pz, pc, pe = split(pos[half, pl.ds(g, 1), :])
@@ -203,98 +210,134 @@
         block = grid[s].reshape(256, 256)
         for tile in range(8):
             d = jnp.dot(block, ut[:, pl.ds(tile * 256, 256)], preferred_element_type=jnp.float32)
-            prob[s, :, pl.ds(tile * 256, 256)] = jnp.exp2(d * SCALE)
+            groups = (tile * 2, tile * 2 + 1)
+            wants = [jnp.broadcast_to(key_ref[g // 8, pl.ds(g % 8, 1), :] - s * 256, (8, 128)) for g in groups]
+            chosen = [hit_ref[:, pl.ds(g * 128, 128)] for g in groups]
+            for k in range(32):
+                row = iota_ref[pl.ds(k * 8, 8), :]
+                for part in range(2):
+                    here = d[k * 8 : k * 8 + 8, part * 128 : part * 128 + 128]
+                    prob[s, pl.ds(k * 8, 8), pl.ds(groups[part] * 128, 128)] = jnp.exp2(here * SCALE)
+                    chosen[part] = jnp.where(row == wants[part], here, chosen[part])
             for part in range(2):
-                g = tile * 2 + part
-                want = jnp.broadcast_to(key_ref[g // 8, pl.ds(g % 8, 1), :] - s * 256, (8, 128))
-                chosen = hit_ref[:, pl.ds(g * 128, 128)]
+                hit_ref[:, pl.ds(groups[part] * 128, 128)] = chosen[part]
+
+    def finish_slots(slots):
+        for n, s in enumerate(slots):
+            fill_ids(idc_ref.at[n], cols_ref, (z - s + 16) & 15, turned(s))
+        for n, s in enumerate(slots):
+            block = grid[s].reshape(256, 256)
+            for tile in range(8):
+                d = jnp.dot(block, ut[:, pl.ds(tile * 256, 256)], preferred_element_type=jnp.float32)
+                groups = (tile * 2, tile * 2 + 1)
+                wants = [jnp.broadcast_to(key_ref[g // 8, pl.ds(g % 8, 1), :] - s * 256, (8, 128)) for g in groups]
+                pids = [jnp.broadcast_to(pid_ref[g // 8, pl.ds(g % 8, 1), :], (8, 128)) for g in groups]
+                chosen = [hit_ref[:, pl.ds(g * 128, 128)] for g in groups]
+                sums = [[acc_ref[:, pl.ds(g * 128, 128)], None] for g in groups]
                 for k in range(32):
-                    here = d[k * 8 : k * 8 + 8, part * 128 : part * 128 + 128]
-                    chosen = jnp.where(iota_ref[pl.ds(k * 8, 8), :] == want, here, chosen)
-                hit_ref[:, pl.ds(g * 128, 128)] = chosen
+                    row = iota_ref[pl.ds(k * 8, 8), :]
+                    ids = idc_ref[n, pl.ds(k * 8, 8), :]
+                    for part in range(2):
+                        here = d[k * 8 : k * 8 + 8, part * 128 : part * 128 + 128]
+                        term = jnp.where(ids == pids[part], 0.0, jnp.exp2(here * SCALE))
+                        old = sums[part][k % 2]
+                        sums[part][k % 2] = term if old is None else old + term
+                        chosen[part] = jnp.where(row == wants[part], here, chosen[part])
+                for part in range(2):
+                    lanes = pl.ds(groups[part] * 128, 128)
+                    hit_ref[:, lanes] = chosen[part]
+                    acc_ref[:, lanes] = sums[part][0] + sums[part][1]
 
     def collect(s):
-        fill_ids(idc_ref, cols_ref, (z - s + 16) & 15, turned(s))
-        for g in range(16):
-            pid = jnp.broadcast_to(pid_ref[g // 8, pl.ds(g % 8, 1), :], (8, 128))
-            sums = [acc_ref[:, pl.ds(g * 128, 128)], None, None, None]
+        fill_ids(idc_ref.at[0], cols_ref, (z - s + 16) & 15, turned(s))
+        for four in range(4):
+            groups = [four * 4 + n for n in range(4)]
+            pids = [jnp.broadcast_to(pid_ref[g // 8, pl.ds(g % 8, 1), :], (8, 128)) for g in groups]
+            sums = [[acc_ref[:, pl.ds(g * 128, 128)], None] for g in groups]
             for k in range(32):
                 rows = pl.ds(k * 8, 8)
-                term = jnp.where(idc_ref[rows, :] == pid, 0.0, prob[s, rows, pl.ds(g * 128, 128)])
-                sums[k % 4] = term if sums[k % 4] is None else sums[k % 4] + term
-            acc_ref[:, pl.ds(g * 128, 128)] = (sums[0] + sums[1]) + (sums[2] + sums[3])
+                ids = idc_ref[0, rows, :]
+                for n, g in enumerate(groups):
+                    term = jnp.where(ids == pids[n], 0.0, prob[s, rows, pl.ds(g * 128, 128)])
+                    sums[n][k % 2] = term if sums[n][k % 2] is None else sums[n][k % 2] + term
+            for n, g in enumerate(groups):
+                acc_ref[:, pl.ds(g * 128, 128)] = sums[n][0] + sums[n][1]
 
     def forward(slots):
         for s in slots:
-            for d in (1, 3, 2):
-                stage2(s, d).wait_recv()
+            sized(grid.at[s, 0, pl.ds(0, 3)], s2, r2.at[s]).wait_recv()
             for d in (1, 3, 2):
                 stage3(s, d).start()
 
     def landed(s):
-        for d in (1, 3, 2):
-            send(grid.at[s, 0], grid.at[s, 0], s3.at[s, d], r3.at[s, d], partner).wait_recv()
+        sized(grid.at[s, pl.ds(0, 3)], s3, r3.at[s]).wait_recv()
 
     def hand_on(s):
         export(s).start()
         export_here(s).start()
 
-    def loop(count, slot_of, step):
+    def loop(first, stop, slot_of, step):
         def turn(i, carry):
             step(slot_of(i))
             return carry
 
-        lax.fori_loop(0, count, turn, 0)
-
-    def early(s):
-        landed(s)
-        hand_on(s)
-        evaluate(s)
-
-    def late_whole(s):
-        send(grid.at[s], grid.at[s], sw.at[s], rw.at[s], partner).wait_recv()
-        hand_on(s)
-        evaluate(s)
-        collect(s)
-
-    def late(s):
-        early(s)
-        collect(s)
+        lax.fori_loop(first, stop, turn, 0)
+
+    def early(slots):
+        for s in slots:
+            landed(s)
+            hand_on(s)
+        for s in slots:
+            evaluate(s)
+
+    def late_whole(slots):
+        for s in slots:
+            sized(grid.at[s], sw, rw.at[mark_whole(s)]).wait_recv()
+            hand_on(s)
+        finish_slots(slots)
+
+    def late(slots):
+        for s in slots:
+            landed(s)
+            hand_on(s)
+        finish_slots(slots)
+
+    def take(slots):
+        for s in slots:
+            stage1(s).wait_recv()
+            for d in (1, 3, 2):
+                stage2(s, d).start()
 
     turn_users()
     forward((0,))
     for s in (4, 12):
+        ids_copy(s).wait_recv()
         stage1(s).wait_recv()
-        ids_copy(s).wait_recv()
     for s in FAR:
         ids_copy(s).start()
         stage1(s).start()
     for s in (4, 12):
         for d in (1, 3, 2):
             stage2(s, d).start()
-    for s in (3, 13):
-        stage1(s).wait_recv()
-        for d in (1, 3, 2):
-            stage2(s, d).start()
+    take((3, 13))
     landed(0)
     for s in WHOLE:
         whole(s).start()
     hand_on(0)
+    take((5, 11, 6, 10))
     evaluate(0)
     forward((4, 12, 3, 13))
     share_ids()
-    for s in FAR:
-        stage1(s).wait_recv()
-        for d in (1, 3, 2):
-            stage2(s, d).start()
-    loop(2, lambda i: 4 + 8 * i, early)
-    forward(FAR[:4])
-    loop(2, lambda i: 3 + 10 * i, early)
-    forward(FAR[4:])
+    take(FAR)
+    early((4, 12))
+    forward((5, 11, 6, 10))
+    early((3, 13))
+    forward(FAR)
     find_ids()
-    loop(5, lambda i: jnp.where(i < 2, i * 4, jnp.where(i == 2, 12, 10 * i - 27)), collect)
-    loop(4, lambda i: jnp.where(i % 2 == 0, 1 + i // 2, 15 - i // 2), late_whole)
-    loop(7, lambda i: 8 + jnp.where(i % 2 == 1, (i + 1) // 2, -(i // 2)), late)
+    loop(0, 5, lambda i: jnp.where(i < 2, i * 4, jnp.where(i == 2, 12, 10 * i - 27)), collect)
+    loop(0, 2, lambda i: (1 + i, 15 - i), late_whole)
+    loop(0, 3, lambda i: (5 + i, 11 - i), late)
+    late((8,))
 
     for half in range(2):
         for g in range(8):
@@ -305,21 +348,14 @@
     last.start()
     for swap in swaps:
         swap.wait_send()
-    for s in range(1, 16):
-        ids_copy(s).wait_send()
-    for s in WHOLE:
-        whole(s).wait_send()
-    for s in NEAR + FAR:
-        stage1(s).wait_send()
-    for s in (0,) + NEAR + FAR:
-        for d in (1, 2, 3):
-            stage2(s, d).wait_send()
-            stage3(s, d).wait_send()
-    for s in range(16):
-        export(s).wait()
-        export_here(s).wait()
-    for n, to in enumerate(across):
-        table_copy(n, *to).wait_send()
+    sized(ids_z.at[pl.ds(0, 15)], si, ri.at[2]).wait_send()
+    sized(grid.at[pl.ds(0, 11), 0, 0], s1, r1.at[3]).wait_send()
+    sized(grid.at[pl.ds(0, 9), 0], s2, r2.at[0]).wait_send()
+    sized(grid.at[pl.ds(0, 9)], s3, r3.at[0]).wait_send()
+    sized(grid.at[pl.ds(0, 4)], sw, rw.at[0]).wait_send()
+    sized(table_ref.at[pl.ds(0, 31)], st, rt).wait_send()
+    send(grid, pool_hbm.at[c], se, re, partner).wait()
+    pltpu.make_async_copy(grid, pool_hbm.at[c], le).wait()
     last.wait()
     chosen = mine_ref[c, 1] + theirs_ref[1]
     others = mine_ref[c, 0] + theirs_ref[0]
@@ -406,18 +442,18 @@
             pltpu.VMEM((8, 2048), f32),
             pltpu.VMEM((8, 2048), f32),
             pltpu.VMEM((2, 256, 128), f32),
-            pltpu.VMEM((256, 128), f32),
+            pltpu.VMEM((2, 256, 128), f32),
             pltpu.VMEM((2, 2, 8, 128), f32),
             pltpu.VMEM((2, 8, 128), f32),
             dma((4,)),
-            dma((16,)), dma((16,)),
-            dma((16, 4)), dma((16, 4)),
-            dma((16, 4)), dma((16, 4)),
-            dma((16,)), dma((16,)),
-            dma((16,)), dma((16,)),
-            dma((31,)), dma((31,)),
+            dma, dma((14,)),
+            dma, dma((14,)),
+            dma, dma((14,)),
+            dma, dma((4,)),
+            dma, dma((3,)),
+            dma, dma,
             dma((2,)), dma((2,)),
-            dma((16,)), dma((16,)), dma((16,)),
+            dma, dma, dma,
             dma, dma,
         ],
         compiler_params=pltpu.CompilerParams(collective_id=0, has_side_effects=True, vmem_limit_bytes=67_000_000),

time: 96.5 us -> 92.3 us (0.956)
  Pallas kernels: 95.6 us -> 91.2 us
    pallas_call x1, Pallas kernels: 46.1 us -> 41.7 us  [body(): pl.pallas_call(gather_kernel, name='gather_scores', out_shape=(jax.ShapeD...]
where the time goes in v4:
time: 92.3 us; the launch traced here: 91.2 us
  Pallas kernels  91.2 us (99%)
    pallas_call x1, Pallas kernels, body(): pl.pallas_call(finish_kernel, name='finish', out_shape=jax.ShapeDtypeStru...  49.5 us
    pallas_call x1, Pallas kernels, body(): pl.pallas_call(gather_kernel, name='gather_scores', out_shape=(jax.ShapeD...  41.7 us

profile of v4, /device:TPU:6, one launch (start us, length us, event | category | flops | bytes accessed | tf_op | source)
XLA Modules:
  0.0 91.2 jit_solution(14131157452355765437)
XLA Ops:
  0.0 41.7 %gather_scores.1 = (f32[4,8,128]{2,1,0:T(8,128)}, f32[32,2,128]{2,1,0:T(2,128)}, bf16[2,16,4,4,16,256]{5,4,3,2,1,0:T(8,128)(2,1)}) custom-call(bf16[1024,256]{1,0:T(8,128)(2,1)} %users_hbm.3, s32[8,128]{1,0:T(8,128)} %bitcast.3, bf16[16,256]{1,0:T(8,128)(2,1)} %items_hbm.1, s32[1,16]{1,0:T(1,128)} %bitcast.4), custom_call_target="tpu_custom_call" | custom-call | tf_op jit(solution)/shard_map/gather_scores/pallas_call | solution.py:420
  41.8 49.5 %finish.1 = f32[8,128]{1,0:T(8,128)} custom-call(f32[4,8,128]{2,1,0:T(8,128)} %get-tuple-element.8.stat_ref, f32[32,2,128]{2,1,0:T(2,128)} %get-tuple-element.9.table_hbm, bf16[1024,256]{1,0:T(8,128)(2,1)} %users_hbm.3, bf16[2,16,4,4,16,256]{5,4,3,2,1,0:T(8,128)(2,1)} %get-tuple-element.10.pool_hbm), custom_call_target="tpu_custom_call" | custom-call | tf_op jit(solution)/shard_map/finish/pallas_call | solution.py:461

commit v5 on v4

--- a/solution.py
+++ b/solution.py
@@ -14,8 +14,8 @@
 START = -1e20
 SMALL = 2.0**-80
 LARGE = 2.0**100
-NEAR = (4, 12, 6, 10, 5, 11, 3, 13)
-FAR = (8, 9, 7)
+NEAR = (4, 12, 3, 13)
+FAR = (8, 9, 7, 10, 6, 11, 5)
 WHOLE = (1, 15, 2, 14)
 
 
@@ -120,7 +120,7 @@
         return (s, x, y) if 8 <= s < 14 else (s, y, x)
 
     def via(s):
-        return 0 if s not in FAR else (12 if s == 9 else 4)
+        return 0 if s not in FAR else (12 if s >= 9 else 4)
 
     def ids_copy(s):
         mark = 0 if s == 4 else (1 if s == 12 else 2)
@@ -324,15 +324,14 @@
     for s in WHOLE:
         whole(s).start()
     hand_on(0)
-    take((5, 11, 6, 10))
     evaluate(0)
     forward((4, 12, 3, 13))
     share_ids()
     take(FAR)
     early((4, 12))
-    forward((5, 11, 6, 10))
+    forward(FAR[:4])
     early((3, 13))
-    forward(FAR)
+    forward(FAR[4:])
     find_ids()
     loop(0, 5, lambda i: jnp.where(i < 2, i * 4, jnp.where(i == 2, 12, 10 * i - 27)), collect)
     loop(0, 2, lambda i: (1 + i, 15 - i), late_whole)

time: 92.3 us -> 91.3 us (0.989)
  Pallas kernels: 91.2 us -> 90.1 us
    pallas_call x1, Pallas kernels: 41.7 us -> 40.6 us  [body(): pl.pallas_call(gather_kernel, name='gather_scores', out_shape=(jax.ShapeD...]
where the time goes in v5:
time: 91.3 us; the launch traced here: 90.2 us
  Pallas kernels  90.1 us (99%)
    pallas_call x1, Pallas kernels, body(): pl.pallas_call(finish_kernel, name='finish', out_shape=jax.ShapeDtypeStru...  49.5 us
    pallas_call x1, Pallas kernels, body(): pl.pallas_call(gather_kernel, name='gather_scores', out_shape=(jax.ShapeD...  40.6 us

profile of v5, /device:TPU:6, one launch (start us, length us, event | category | flops | bytes accessed | tf_op | source)
XLA Modules:
  0.0 90.2 jit_solution(14121358838742088762)
XLA Ops:
  0.0 40.6 %gather_scores.1 = (f32[4,8,128]{2,1,0:T(8,128)}, f32[32,2,128]{2,1,0:T(2,128)}, bf16[2,16,4,4,16,256]{5,4,3,2,1,0:T(8,128)(2,1)}) custom-call(bf16[1024,256]{1,0:T(8,128)(2,1)} %users_hbm.3, s32[8,128]{1,0:T(8,128)} %bitcast.3, bf16[16,256]{1,0:T(8,128)(2,1)} %items_hbm.1, s32[1,16]{1,0:T(1,128)} %bitcast.4), custom_call_target="tpu_custom_call" | custom-call | tf_op jit(solution)/shard_map/gather_scores/pallas_call | solution.py:419
  40.7 49.5 %finish.1 = f32[8,128]{1,0:T(8,128)} custom-call(f32[4,8,128]{2,1,0:T(8,128)} %get-tuple-element.8.stat_ref, f32[32,2,128]{2,1,0:T(2,128)} %get-tuple-element.9.table_hbm, bf16[1024,256]{1,0:T(8,128)(2,1)} %users_hbm.3, bf16[2,16,4,4,16,256]{5,4,3,2,1,0:T(8,128)(2,1)} %get-tuple-element.10.pool_hbm), custom_call_target="tpu_custom_call" | custom-call | tf_op jit(solution)/shard_map/finish/pallas_call | solution.py:460
